TPU v7x, 8 devices: a whole 2x2x1 slice. The times are simulated.
8 devices in a mesh: dp: 2 (over z, y), cp: 4 (over x, core).
Axes of the slice: x: 2, y: 2, z: 1, core: 2. Of those that a mesh axis runs over, the one named last changes fastest.
Arguments:
- x: bfloat16 [128, 2560], P('dp'), parts along dimension 0
- w_dq: bfloat16 [2560, 768], replicated
- g_q: float32 [768], replicated
- w_uq: bfloat16 [768, 3840], replicated
- w_dkv: bfloat16 [2560, 288], replicated
- g_kv: float32 [256], replicated
- w_uk: bfloat16 [256, 40, 64], replicated
- w_uv: bfloat16 [256, 40, 64], replicated
- w_o: bfloat16 [2560, 2560], replicated
- cache_c: bfloat16 [128, 16384, 256], P('dp', 'cp'), parts along dimension 0
- cache_kr: bfloat16 [128, 16384, 32], P('dp', 'cp'), parts along dimension 0
- ctx_len: int32 [128], P('dp'), parts along dimension 0
Outputs:
- output 1: bfloat16 [128, 2560], P('dp'), parts along dimension 0
- output 2: bfloat16 [128, 256], P('dp'), parts along dimension 0
- output 3: bfloat16 [128, 32], P('dp'), parts along dimension 0
There are 2 independent parts. A program takes and returns all parts, laid end to end along the dimension named above; an argument that names none is the same for every part.
All inputs are finite; a program needn't handle non-finite values.
Results may differ from a plain program's by a relative error of at most 0.00630591.
Values sent between devices are 32-bit elements.
A program may use at most 1 GiB of HBM per device.

v0:
```python
import jax
import jax.numpy as jnp
from jax import lax
from jax.sharding import PartitionSpec as P, NamedSharding

NORM_EPS = 1e-6
ROPE_THETA = 10000.0
MASKED = -1e30


def rms_norm(values, gain_vec):
    mean_sq = jnp.mean(jnp.square(values), axis=-1, keepdims=True)
    return values * lax.rsqrt(mean_sq + NORM_EPS) * gain_vec


def rope_tables(positions, rope_dim):
    half_dim = rope_dim // 2
    inv_freq = ROPE_THETA ** (-2.0 * jnp.arange(half_dim, dtype=jnp.float32) / rope_dim)
    angles = positions.astype(jnp.float32)[..., None] * inv_freq
    return jnp.cos(angles), jnp.sin(angles)


def rope_rotate(values, cos_tab, sin_tab):
    half_dim = values.shape[-1] // 2
    lo_half = values[..., :half_dim]
    hi_half = values[..., half_dim:]
    return jnp.concatenate([lo_half * cos_tab - hi_half * sin_tab, hi_half * cos_tab + lo_half * sin_tab], axis=-1)


def project_step(x, w_dq, g_q, w_uq, w_dkv, g_kv, w_uk, ctx_len):
    n_req = x.shape[0]
    latent, n_heads, nope_dim = w_uk.shape
    rope_dim = w_dkv.shape[1] - latent
    cq_low = jnp.dot(x, w_dq, preferred_element_type=jnp.float32).astype(jnp.bfloat16)
    cq_norm = rms_norm(cq_low.astype(jnp.float32), g_q).astype(jnp.bfloat16)
    q_full = jnp.dot(cq_norm, w_uq, preferred_element_type=jnp.float32).astype(jnp.bfloat16)
    q_full = q_full.reshape(n_req, n_heads, nope_dim + rope_dim)
    cos_tab, sin_tab = rope_tables(ctx_len, rope_dim)
    q_rope = rope_rotate(q_full[:, :, nope_dim:].astype(jnp.float32), cos_tab[:, None, :], sin_tab[:, None, :]).astype(jnp.bfloat16)
    q_lat = jnp.einsum('bhn,khn->bhk', q_full[:, :, :nope_dim], w_uk, preferred_element_type=jnp.float32).astype(jnp.bfloat16)
    kv_full = jnp.dot(x, w_dkv, preferred_element_type=jnp.float32)
    c_new = rms_norm(kv_full[:, :latent], g_kv).astype(jnp.bfloat16)
    kr_new = rope_rotate(kv_full[:, latent:], cos_tab, sin_tab).astype(jnp.bfloat16)
    return q_lat, q_rope, c_new, kr_new


def block_partials(q_lat, q_rope, c_new, kr_new, cache_c, cache_kr, ctx_len, shard_idx, score_scale):
    t_dev = cache_c.shape[1]
    scores = (jnp.einsum('bhk,btk->bht', q_lat, cache_c, preferred_element_type=jnp.float32)
              + jnp.einsum('bhr,btr->bht', q_rope, cache_kr, preferred_element_type=jnp.float32)) * score_scale
    positions = shard_idx * t_dev + jnp.arange(t_dev)
    valid_pos = positions[None, None, :] < ctx_len[:, None, None]
    scores = jnp.where(valid_pos, scores, MASKED)
    is_owner = ((ctx_len // t_dev) == shard_idx)[:, None]
    new_score = (jnp.einsum('bhk,bk->bh', q_lat, c_new, preferred_element_type=jnp.float32)
                 + jnp.einsum('bhr,br->bh', q_rope, kr_new, preferred_element_type=jnp.float32)) * score_scale
    new_score = jnp.where(is_owner, new_score, MASKED)
    row_max = jnp.maximum(jnp.max(scores, axis=2), new_score)
    weights = jnp.where(valid_pos, jnp.exp(scores - row_max[:, :, None]), 0.0)
    new_weight = jnp.where(is_owner, jnp.exp(new_score - row_max), 0.0)
    row_sum = jnp.sum(weights, axis=2) + new_weight
    lat_acc = jnp.einsum('bht,btk->bhk', weights.astype(jnp.bfloat16), cache_c, preferred_element_type=jnp.float32)
    lat_acc = lat_acc + new_weight.astype(jnp.bfloat16).astype(jnp.float32)[:, :, None] * c_new.astype(jnp.float32)[:, None, :]
    return row_max, row_sum, lat_acc


def output_step(x, o_lat, w_uv, w_o):
    o_heads = jnp.einsum('bhk,khv->bhv', o_lat, w_uv, preferred_element_type=jnp.float32).astype(jnp.bfloat16)
    attn_out = jnp.dot(o_heads.reshape(x.shape[0], -1), w_o, preferred_element_type=jnp.float32)
    return (x.astype(jnp.float32) + attn_out).astype(jnp.bfloat16)


def solution(mesh):
    def decode_step(x, w_dq, g_q, w_uq, w_dkv, g_kv, w_uk, w_uv, w_o, cache_c, cache_kr, ctx_len):
        score_scale = (w_uk.shape[2] + cache_kr.shape[2]) ** -0.5
        shard_idx = lax.axis_index('cp')
        q_lat, q_rope, c_new, kr_new = project_step(x, w_dq, g_q, w_uq, w_dkv, g_kv, w_uk, ctx_len)
        row_max, row_sum, lat_acc = block_partials(q_lat, q_rope, c_new, kr_new, cache_c, cache_kr, ctx_len, shard_idx, score_scale)
        packed = jnp.concatenate([row_max[:, :, None], row_sum[:, :, None], lat_acc], axis=2)
        gathered = lax.all_gather(packed, 'cp')
        block_max = gathered[:, :, :, 0]
        glob_max = jnp.max(block_max, axis=0)
        factor = jnp.exp(block_max - glob_max[None])
        mass_sum = jnp.sum(factor * gathered[:, :, :, 1], axis=0)
        lat_sum = jnp.sum(factor[:, :, :, None] * gathered[:, :, :, 2:], axis=0)
        o_lat = (lat_sum / mass_sum[:, :, None]).astype(jnp.bfloat16)
        return output_step(x, o_lat, w_uv, w_o), c_new, kr_new

    spec_rows = P('dp', None)
    spec_cache = P('dp', 'cp', None)
    in_specs = (spec_rows, P(), P(), P(), P(), P(), P(), P(), P(), spec_cache, spec_cache, P('dp'))
    out_specs = (spec_rows, spec_rows, spec_rows)
    return jax.shard_map(decode_step, mesh=mesh, in_specs=in_specs, out_specs=out_specs, check_vma=False)
```

profile of v0, /device:TPU:0, one launch (start us, length us, event | category | flops | bytes accessed | tf_op | source)
XLA Modules:
  0.0 359.9 jit_solution(126888206994313305)
XLA Ops:
  7.3 1.3 copy-done
  8.5 1.6 fusion.41
  10.3 0.7 convert_element_type.64
  11.0 0.7 fusion.32
  12.2 3.1 multiply_reduce_fusion
  15.4 0.2 broadcast_compare_fusion
  15.6 3.9 %convolution_convert_fusion = bf16[64,3840]{1,0:T(8,128)(2,1)S(1)} fusion(bf16[768,3840]{1,0:T(8,128)(2,1)} %param.15, f32[64,768]{1,0:T(8,128)S(1)} %get-tuple-element.40, f32[768]{0:T(1024)S(1)} %copy-done.9, f32[64]{0:T(128)S(1)} %add_rsqrt_fusion.1), kind=kOutput, calls=%fused_computation.12 | convolution fusion | flops 377880576 | bytes 6589696 | tf_op jit(solution)/shard_map/dot_general | solution.py:36
  19.5 1.0 reshape.119
  20.5 0.2 slice.44
  20.8 0.3 copy.123
  21.2 0.3 subtract_convert_fusion
  21.5 0.2 fusion.24
  21.8 19.7 %fusion.25 = f32[64,40,4096]{2,1,0:T(8,128)} fusion(bf16[64,4096,32]{1,2,0:T(8,128)(2,1)} %param.22, bf16[64,40,16]{1,2,0:T(8,128)(2,1)S(1)} %get-tuple-element.32, bf16[64,40,16]{1,2,0:T(8,128)(2,1)S(1)} %get-tuple-element.31), kind=kOutput, calls=%fused_computation.35 | convolution fusion | flops 671416320 | bytes 58884096 | tf_op jit(solution)/shard_map/bhr,btr->bht/dot_general | solution.py:50
  41.6 1.8 fusion.13
  43.4 0.8 fusion.18
  44.3 71.8 %fusion.6 = (f32[64,40]{1,0:T(8,128)S(1)}, f32[64,40,4096]{2,1,0:T(8,128)}) fusion(f32[64,40,4096]{2,1,0:T(8,128)} %fusion.25, pred[64,4096]{1,0:T(8,128)(4,1)S(1)} %broadcast_compare_fusion, bf16[64,4096,256]{2,1,0:T(8,128)(2,1)} %param.21, bf16[64,40,256]{2,0,1:T(8,128)(2,1)S(1)} %fusion.13), kind=kOutput, calls=%fused_computation.7 | convolution fusion | flops 5410649600 | bytes 219686912 | tf_op jit(solution)/shard_map/bhk,btk->bht/dot_general | solution.py:49
  116.2 26.7 %fusion.1 = f32[64,40]{1,0:T(8,128)S(1)} fusion(f32[64,40]{1,0:T(8,128)S(1)} %fusion.31, f32[64,40,4096]{2,1,0:T(8,128)} %get-tuple-element.42, f32[64,40,4096]{2,1,0:T(8,128)} %fusion.25, pred[64,4096]{1,0:T(8,128)(4,1)S(1)} %broadcast_compare_fusion), kind=kLoop, calls=%fused_computation.3 | loop fusion | flops 62912000 | bytes 84168704 | tf_op jit(solution)/shard_map/reduce_sum | solution.py:61
  143.0 0.5 copy.107
  143.5 0.5 copy.106
  144.0 67.7 %multiply_add_fusion = f32[64,40,256]{2,1,0:T(8,128)} fusion(bf16[64,4096,256]{2,1,0:T(8,128)(2,1)} %param.21, f32[64,40]{1,0:T(8,128)S(1)} %fusion.31, f32[64,40,4096]{2,1,0:T(8,128)} %get-tuple-element.42, f32[64,40,4096]{2,1,0:T(8,128)} %fusion.25, pred[64,4096]{1,0:T(8,128)(4,1)S(1)} %broadcast_compare_fusion, f32[64,256]{1,0:T(8,128)S(1)} %get-tuple-element.26, ...), kind=kOutput, calls=%fused_computation.17 | convolution fusion | flops 5432934400 | bytes 221073408 | tf_op jit(solution)/shard_map/bht,btk->bhk/dot_general | solution.py:62
  211.7 5.4 %pad_maximum_fusion = f32[64,40,258]{2,1,0:T(8,128)} fusion(f32[64,40,256]{2,1,0:T(8,128)} %multiply_add_fusion, f32[64,40,1]{2,1,0:T(8,128)S(1)} %copy.107, f32[64,40,1]{2,1,0:T(8,128)S(1)} %copy.106), kind=kLoop, calls=%fused_computation.13 | loop fusion | flops 1320960 | bytes 5283840 | tf_op jit(solution)/shard_map/concatenate | solution.py:79
  217.1 0.6 pad_maximum_fusion.4
  217.7 100.5 %all-gather.3.cloned.1.call-done = f32[256,40,258]{2,1,0:T(8,128)} async-done(((f32[64,40,258]{2,1,0:T(8,128)}), f32[256,40,258]{2,1,0:T(8,128)}) %all-gather.3.cloned.1.call-update) | async-done | bytes 10567696 | tf_op jit(solution)/shard_map/all_gather | solution.py:80
  318.2 9.7 %fusion.39 = (f32[4,64,40,1]{3,2,1,0:T(8,128)}, f32[64,40]{1,0:T(8,128)S(1)}, f32[4,64,40,1]{3,2,1,0:T(8,128)}) fusion(f32[4,64,40,258]{3,2,1,0:T(8,128)} %bitcast.42), kind=kLoop, calls=%fused_computation.74 | loop fusion | flops 7680 | bytes 174080 | tf_op jit(solution)/shard_map/slice | solution.py:84
  327.9 3.5 copy.110
  331.4 3.5 copy.126
  335.2 8.2 %fusion.9 = f32[64,40,256]{2,1,0:T(8,128)S(1)} fusion(f32[4,64,40,258]{3,2,1,0:T(8,128)} %bitcast.43, f32[4,64,40]{2,1,0:T(8,128)S(1)} %copy.109), kind=kLoop, calls=%fused_computation.11 | loop fusion | flops 4587520 | bytes 13148160 | tf_op jit(solution)/shard_map/reduce_sum | solution.py:85
  343.4 0.4 divide_convert_fusion
  343.8 0.5 fusion.15
  344.3 0.4 copy.113
  344.8 0.4 reshape.120
  345.2 7.9 %fusion.10 = bf16[64,2560]{1,0:T(8,128)(2,1)} fusion(bf16[64,2560]{1,0:T(8,128)(2,1)S(1)} %reshape.120, bf16[2560,2560]{1,0:T(8,128)(2,1)} %param.20, bf16[64,2560]{1,0:T(8,128)(2,1)S(1)} %copy-done.2), kind=kOutput, calls=%fused_computation.15 | convolution fusion | flops 839352320 | bytes 14090240 | tf_op jit(solution)/shard_map/dot_general | solution.py:69
  (48 shorter events, 1.5 us)
Async XLA Ops:
  7.2 1.4 copy-start
  7.2 8.2 %copy-start.11 = (s32[64]{0:T(128)S(1)}, s32[64]{0:T(128)}, u32[]{:S(2)}) copy-start(s32[64]{0:T(128)} %param.23) | copy-start | bytes 772
  7.2 8.4 %copy-start.9 = (f32[768]{0:T(1024)S(1)}, f32[768]{0:T(1024)}, u32[]{:S(2)}) copy-start(f32[768]{0:T(1024)} %param.14) | copy-start | bytes 9220
  7.2 311.0 %all-gather.3.cloned.1.call-start = ((), (), s32[]{:S(2)}) async-start(), calls=%async_computation | async-start | bytes 19660800 | tf_op jit(solution)/shard_map/all_gather | solution.py:80
  11.9 8.6 %copy-start.4 = (bf16[64,16]{0,1:T(8,128)(2,1)}, bf16[64,16]{0,1:T(8,128)(2,1)S(1)}, u32[]{:S(2)}) copy-start(bf16[64,16]{0,1:T(8,128)(2,1)S(1)} %get-tuple-element.35) | copy-start | bytes 6148
  11.9 8.6 %copy-start.6 = (bf16[64,16]{0,1:T(8,128)(2,1)}, bf16[64,16]{0,1:T(8,128)(2,1)S(1)}, u32[]{:S(2)}) copy-start(bf16[64,16]{0,1:T(8,128)(2,1)S(1)} %get-tuple-element.36) | copy-start | bytes 6148
  21.8 19.7 %copy-start.10 = (f32[256]{0:T(256)S(1)}, f32[256]{0:T(256)}, u32[]{:S(2)}) copy-start(f32[256]{0:T(256)} %param.17) | copy-start | bytes 3076
  41.6 1.8 copy-start.8
  211.7 5.4 %copy-start.5 = (bf16[64,16]{0,1:T(8,128)(2,1)S(1)}, bf16[64,16]{0,1:T(8,128)(2,1)}, u32[]{:S(2)}) copy-start(bf16[64,16]{0,1:T(8,128)(2,1)} %copy-done.4) | copy-start | bytes 6148
  211.7 5.5 %copy-start.7 = (bf16[64,16]{0,1:T(8,128)(2,1)S(1)}, bf16[64,16]{0,1:T(8,128)(2,1)}, u32[]{:S(2)}) copy-start(bf16[64,16]{0,1:T(8,128)(2,1)} %copy-done.6) | copy-start | bytes 6148
  335.2 8.7 %copy-start.3 = (bf16[256,40,64]{0,2,1:T(8,128)(2,1)S(1)}, bf16[256,40,64]{0,2,1:T(8,128)(2,1)}, u32[]{:S(2)}) copy-start(bf16[256,40,64]{0,2,1:T(8,128)(2,1)} %param.19) | copy-start | bytes 3932164
  343.4 1.8 copy-start.2
  344.8 8.3 %copy-start.1 = (bf16[2560,288]{0,1:T(8,128)(2,1)S(1)}, bf16[2560,288]{0,1:T(8,128)(2,1)}, u32[]{:S(2)}) copy-start(bf16[2560,288]{0,1:T(8,128)(2,1)} %param.16) | copy-start | bytes 4423684
Sparse Core Ops, SparseCore 0:
  217.2 100.9 all-gather.2
where the time goes:
time: 360 us
  matrix products  179 us (50%)
  waiting for transfers between devices  101 us (28%)
  other arithmetic  53.6 us (15%)
  between operations  14.4 us (4%)
  local copies, waits for them, and re-layouts  12.4 us (3%)
    all_gather x1, waiting for transfers between devices, decode_step(): gathered = lax.all_gather(packed, 'cp')  100 us
    dot_general x1, matrix products, block_partials(): jnp.einsum('bhk,btk->bht', q_lat, cache_c, preferred_element_type=jnp.flo...  71.8 us
    dot_general x1, matrix products, block_partials(): jnp.einsum('bht,btk->bhk', weights.astype(jnp.bfloat16), cache_c, preferr...  67.7 us
    reduce_sum x1, other arithmetic, block_partials(): row_sum = jnp.sum(weights, axis=2) + new_weight  26.7 us
    dot_general x1, matrix products, block_partials(): jnp.einsum('bhr,btr->bht', q_rope, cache_kr, preferred_element_type=jnp.f...  19.7 us
    slice x1, other arithmetic, decode_step(): mass_sum = jnp.sum(factor * gathered[:, :, :, 1], axis=0)  9.68 us
    reduce_sum x1, other arithmetic, decode_step(): lat_sum = jnp.sum(factor[:, :, :, None] * gathered[:, :, :, 2:], axis=0)  8.22 us
    dot_general x1, matrix products, output_step(): jnp.dot(o_heads.reshape(x.shape[0], -1), w_o, preferred_element_type=jnp....  7.86 us
  transfers between devices with their start and end apart: 1, of which 1 were waited for; matrix products, arithmetic and copies ran while one was open for 0% of the time, Pallas kernels for 0%

commit v1 on v0

v1 whole, which is shorter than its diff:
```python
import functools

import jax
import jax.numpy as jnp
import numpy as np
from jax import lax
from jax.experimental import pallas as pl
from jax.experimental.pallas import tpu as pltpu
from jax.sharding import PartitionSpec as P

F32, BF16 = jnp.float32, jnp.bfloat16
NORM_EPS = 1e-6
SCALE = np.float32(96 ** -0.5 * np.log2(np.e))
MASKED = -2.0e38
FLOOR = -1.0e38

NREQ, T, H, L, R, D, QL = 64, 4096, 40, 256, 32, 2560, 768
HP = 48
NT = 8
NB = 8
NOWN = NREQ // 2
LEAD = 3
NCT = 8
XPOSE_TILES = ((1, 0), (0, 0))


def decode_kernel(x_ref, gq_ref, gkv_ref, freq_ref, ctxv_ref, ctx_ref, wdq_h, wuq_h, wdkv_h, wuk_h, wuv_h, wo_h, c_h, kr_h,
                  xo_ref, co_ref, ko_ref,
                  wdq, wuq, wdkv, wuk, wuv, wo, cbuf, krbuf, qf, qrf, qb, qrb, cnf, krf,
                  sbuf, mbuf, ctb, send_a, recv_1, own_b, send_b, recv_2, ola, olb, xbuf,
                  wsem, csem, ksem, sa_sem, r1_sem, sb_sem, r2_sem, xs_sem, xr_sem):
    cp = lax.axis_index('cp')
    core = lax.rem(cp, 2)
    sibling = cp + 1 - 2 * core
    mirror = lax.rem(cp + 2, 4)

    barrier = pltpu.get_barrier_semaphore()
    for other in (sibling, mirror):
        pl.semaphore_signal(barrier, inc=1, device_id={'cp': other}, device_id_type=pl.DeviceIdType.MESH)

    weights = [pltpu.make_async_copy(h, v, wsem.at[k]) for k, (h, v) in enumerate(
        ((wdq_h, wdq), (wdkv_h, wdkv), (wuq_h, wuq), (wuk_h, wuk), (wuv_h, wuv), (wo_h, wo)))]

    def request(s):
        u = lax.rem(s, 2)
        half = (1 - core) * (1 - u) + core * u
        return half * NOWN + s // 2

    def cache_copies(s):
        b, slot = request(s), lax.rem(s, NB)
        return (pltpu.make_async_copy(c_h.at[b], cbuf.at[slot], csem.at[slot]),
                pltpu.make_async_copy(kr_h.at[b], krbuf.at[slot], ksem.at[slot]))

    def start(s):
        for copy in cache_copies(s):
            copy.start()

    def wait(s):
        for copy in cache_copies(s):
            copy.wait()

    for copy in weights[:4]:
        copy.start()
    for s in range(NB):
        start(s)

    lane128 = lax.broadcasted_iota(jnp.int32, (1, 128), 1)
    lane256 = lax.broadcasted_iota(jnp.int32, (1, 256), 1)

    dot = functools.partial(jnp.dot, preferred_element_type=F32)
    dot_t = functools.partial(lax.dot_general, dimension_numbers=(((1,), (1,)), ((), ())), preferred_element_type=F32)

    angle = ctxv_ref[...].astype(F32) * freq_ref[...]
    cos_t = jnp.cos(angle)
    sin_t = jnp.sin(angle) * jnp.where(lax.rem(lane128, 32) < 16, -1.0, 1.0)

    weights[0].wait()
    cq = [dot(x_ref[...], wdq[:, n * 256:(n + 1) * 256]).astype(BF16).astype(F32) for n in range(3)]
    mean_sq = sum(jnp.sum(v * v, axis=1, keepdims=True) for v in cq) * np.float32(1.0 / QL)
    inv_q = lax.rsqrt(mean_sq + NORM_EPS)
    cn = jnp.concatenate([(cq[n] * inv_q * gq_ref[:, n * 256:(n + 1) * 256]).astype(BF16) for n in range(3)], axis=1)

    weights[1].wait()
    kv = dot_t(x_ref[...], wdkv[:L, :])
    inv_kv = lax.rsqrt(jnp.sum(kv * kv, axis=1, keepdims=True) * np.float32(1.0 / L) + NORM_EPS)
    c_new = (kv * inv_kv * gkv_ref[...]).astype(BF16)
    co_ref[...] = c_new
    cnf[...] = c_new.astype(F32)
    kr = dot_t(x_ref[...], wdkv[L:L + R, :])
    kr = jnp.concatenate([kr, jnp.zeros((NREQ, 128 - R), F32)], axis=1)
    partner = jnp.where(lane128 < 16, pltpu.roll(kr, 112, 1), pltpu.roll(kr, 16, 1))
    kr_new = (kr * cos_t + partner * sin_t).astype(BF16)
    ko_ref[...] = kr_new[:, :R]
    krf[...] = jnp.where(lane128 < R, kr_new.astype(F32), 0.0)

    weights[2].wait()
    for n in range(15):
        qf[:, n * 256:(n + 1) * 256] = dot(cn, wuq[:, n * 256:(n + 1) * 256]).astype(BF16)

    row = lax.broadcasted_iota(jnp.int32, (256, 256), 0)
    col = lax.broadcasted_iota(jnp.int32, (256, 256), 1)
    src = lax.rem(col + jnp.where(col < 128, 0, 16), 32)
    for o in range(8):
        pick = jnp.where(row == src + 32 * o, 1.0, 0.0).astype(BF16)
        heads = [h for h in range(H) if ((96 * h + 64) % 256) // 32 == o]
        wins = [(96 * h + 64) // 256 for h in heads]
        both = dot(jnp.concatenate([qf[:, w * 256:(w + 1) * 256] for w in wins], axis=0), pick)
        for k, h in enumerate(heads):
            part = both[k * NREQ:(k + 1) * NREQ]
            qrf[pl.ds(h, NREQ, stride=H), :] = (part[:, :128] * cos_t + part[:, 128:] * sin_t).astype(BF16).astype(F32)

    weights[3].wait()
    nope = {h: (96 * h, 96 * h + 64) for h in range(H)}
    carry = {}
    for w in range(15):
        lo, hi = 256 * w, 256 * (w + 1)
        here = [(h, max(a, lo), min(b, hi)) for h, (a, b) in nope.items() if a < hi and b > lo]
        pieces, at = [], lo
        for h, a, b in here:
            if a > at:
                pieces.append(jnp.zeros((a - at, 256), BF16))
            pieces.append(wuk[h, a - nope[h][0]:b - nope[h][0], :])
            at = b
        if at < hi:
            pieces.append(jnp.zeros((hi - at, 256), BF16))
        window = qf[:, lo:hi]
        lhs = [window * jnp.where((lane256 >= a - lo) & (lane256 < b - lo), 1.0, 0.0).astype(BF16) for _, a, b in here]
        lat = dot(jnp.concatenate(lhs, axis=0), jnp.concatenate(pieces, axis=0))
        for k, (h, a, b) in enumerate(here):
            v = lat[k * NREQ:(k + 1) * NREQ]
            if a > nope[h][0]:
                v = v + carry.pop(h)
            if b < nope[h][1]:
                carry[h] = v
                continue
            v = v.astype(BF16).astype(F32)
            ola[pl.ds(h, NREQ, stride=H), :] = v[:, :128]
            olb[pl.ds(h, NREQ, stride=H), :] = v[:, 128:]
    pl.semaphore_wait(barrier, 2)

    def to_bf16(b, _):
        rows = pl.ds(pl.multiple_of(b * H, 8), H)
        qb[b] = jnp.concatenate([jnp.concatenate([ola[rows, :], olb[rows, :]], axis=1), jnp.zeros((HP - H, L), F32)], axis=0).astype(BF16)
        qrb[b] = jnp.concatenate([qrf[rows, :], jnp.zeros((HP - H, 128), F32)], axis=0).astype(BF16)
        return 0
    lax.fori_loop(0, NREQ, to_bf16, 0)

    def rcopy_1(i):
        return pltpu.make_async_remote_copy(src_ref=send_a.at[i], dst_ref=recv_1.at[i], send_sem=sa_sem.at[i], recv_sem=r1_sem.at[i],
                                            device_id={'cp': sibling}, device_id_type=pl.DeviceIdType.MESH)

    def rcopy_2(i):
        return pltpu.make_async_remote_copy(src_ref=send_b.at[i], dst_ref=recv_2.at[i], send_sem=sb_sem.at[i], recv_sem=r2_sem.at[i],
                                            device_id={'cp': mirror}, device_id_type=pl.DeviceIdType.MESH)

    def put_partial(ref, i, lo, hi, m, l):
        ref[i, 0:H, :] = lo
        ref[i, H:2 * H, :] = hi
        ml = jnp.zeros((8, 128), F32)
        for g in range(5):
            ml = jnp.where(lane128 == g, m[8 * g:8 * g + 8], ml)
            ml = jnp.where(lane128 == 8 + g, l[8 * g:8 * g + 8], ml)
        ref[i, 2 * H:2 * H + 8, :] = ml

    def get_partial(ref, i):
        ml = ref[i, 2 * H:2 * H + 8, :]
        spread = lambda at: jnp.concatenate([jnp.broadcast_to(ml[:, at + g:at + g + 1], (8, 128)) for g in range(5)], axis=0)
        return ref[i, 0:H, :], ref[i, H:2 * H, :], spread(0), spread(8)

    def combine_1(i):
        lo_p, hi_p, m_p, l_p = get_partial(own_b, i)
        lo_q, hi_q, m_q, l_q = get_partial(recv_1, i)
        m = jnp.maximum(m_p, m_q)
        f_p, f_q = jnp.exp2(m_p - m), jnp.exp2(m_q - m)
        put_partial(send_b, i, lo_p * f_p + lo_q * f_q, hi_p * f_p + hi_q * f_q, m, l_p * f_p + l_q * f_q)

    def combine_2(i):
        lo_p, hi_p, m_p, l_p = get_partial(send_b, i)
        lo_q, hi_q, m_q, l_q = get_partial(recv_2, i)
        ii = jnp.minimum(i, NOWN - 1)
        b = core * NOWN + ii
        c_row, k_row = cnf[pl.ds(b, 1), :], krf[pl.ds(b, 1), :]
        q, qr = qb[b].astype(F32)[:H], qrb[b].astype(F32)[:H]
        part = q[:, :128] * c_row[:, :128] + q[:, 128:] * c_row[:, 128:] + qr * k_row
        s_new = jnp.broadcast_to(jnp.sum(part, axis=1, keepdims=True) * SCALE, (H, 128))
        m = jnp.maximum(jnp.maximum(m_p, m_q), s_new)
        f_p, f_q, w_new = jnp.exp2(m_p - m), jnp.exp2(m_q - m), jnp.exp2(s_new - m)
        inv = 1.0 / (l_p * f_p + l_q * f_q + w_new)
        w_new = w_new.astype(BF16).astype(F32)
        rows = pl.ds(pl.multiple_of(i * H, 8), H)
        ola[rows, :] = (lo_p * f_p + lo_q * f_q + w_new * c_row[:, :128]) * inv
        olb[rows, :] = (hi_p * f_p + hi_q * f_q + w_new * c_row[:, 128:]) * inv

    def attend():
        count = [0]

        def qk_tile(s, par, j, mx):
            slot, b = lax.rem(s, NB), request(s)
            n = ctx_ref[b] - cp * T
            at = pl.ds(256 * j, 256)
            c = cbuf[slot, at, :]
            if (par, j // 2) in XPOSE_TILES:
                v = dot_t(qb[b], c)
            else:
                t = count[0] % NCT
                count[0] += 1
                ctb[t] = c.T
                v = dot(qb[b], ctb[t])
            v = (v + dot(qrb[b][:, :R], krbuf[slot, :, at]))[:H]
            v = jnp.where(lane256 + j * 256 < n, v, MASKED)
            sbuf[par, :, at] = v
            for k in range(2):
                part = v[:, k * 128:(k + 1) * 128]
                mx = part if mx is None else jnp.maximum(mx, part)
            return mx

        def pv_tile(s, par, j, mk, st):
            ws = []
            for k in range(2):
                w = jnp.exp2(sbuf[par, :, pl.ds(j * 256 + k * 128, 128)] * SCALE - mk)
                st['l'] = w if st['l'] is None else st['l'] + w
                ws.append(w)
            w = jnp.concatenate([jnp.concatenate(ws, axis=1), jnp.zeros((HP - H, 256), F32)], axis=0).astype(BF16)
            p = dot(w, cbuf[lax.rem(s, NB), pl.ds(256 * j, 256), :])
            st[j % 2] = p if st[j % 2] is None else st[j % 2] + p

        def half(s, par, out, out_i, last=False):
            mk = jnp.broadcast_to(jnp.maximum(jnp.max(mbuf[par], axis=1, keepdims=True), FLOOR) * SCALE, (H, 128))
            mx, st = None, {0: None, 1: None, 'l': None}
            for j in range(2 * (NT + LEAD)):
                if not last and j < 2 * NT:
                    mx = qk_tile(s + 1, 1 - par, j, mx)
                if j >= 2 * LEAD:
                    pv_tile(s, par, j - 2 * LEAD, mk, st)
            if not last:
                mbuf[1 - par] = mx
            a = (st[0] + st[1])[:H]
            l = jnp.broadcast_to(jnp.sum(st['l'], axis=1, keepdims=True), (H, 128))
            put_partial(out, out_i, a[:, :128], a[:, 128:], mk, l)

        for ref in (own_b, recv_1, send_b, recv_2):
            ref[NOWN] = jnp.zeros((2 * H + 8, 128), F32)

        wait(0)
        mx = None
        for j in range(2 * NT):
            mx = qk_tile(0, 0, j, mx)
        mbuf[0] = mx

        def trip(i, last=False):
            s = 2 * i
            wait(s + 1)
            if not last:
                wait(s + 2)

            def when(lag, act):
                if isinstance(i, int):
                    if i >= lag:
                        act()
                else:
                    pl.when(i >= lag)(act)
            when(1, lambda: rcopy_1(i - 1).start())
            when(2, lambda: rcopy_1(i - 2).wait_recv())
            when(3, lambda: rcopy_2(i - 3).start())
            when(6, lambda: rcopy_2(i - 6).wait_recv())
            lagged = lambda lag: jnp.where(i >= lag, i - lag, NOWN)
            half(s, 0, send_a, i)
            combine_1(lagged(2))
            half(s + 1, 1, own_b, i, last=last)
            combine_2(lagged(6))

        def loop_trip(i, _):
            trip(i)
            for u in range(2):
                s = 2 * i + u
                pl.when(s + NB < NREQ)(lambda s=s: start(s + NB))

            @pl.when(i == NREQ // 2 - NB // 2)
            def _():
                for copy in weights[4:]:
                    copy.start()
            return 0
        lax.fori_loop(0, NOWN - 1, loop_trip, 0)
        trip(NOWN - 1, last=True)
        rcopy_1(NOWN - 1).start()
        rcopy_1(NOWN - 2).wait_recv()
        combine_1(NOWN - 2)
        rcopy_2(NOWN - 3).start()
        rcopy_1(NOWN - 1).wait_recv()
        rcopy_2(NOWN - 2).start()
        combine_1(NOWN - 1)
        for i in range(NOWN - 6, NOWN - 3):
            rcopy_2(i).wait_recv()
            if i == NOWN - 6:
                rcopy_2(NOWN - 1).start()
            combine_2(i)
        for i in range(NOWN - 3, NOWN):
            rcopy_2(i).wait_recv()
            combine_2(i)

    attend()

    def output():
        weights[4].wait()
        groups = []
        for g in range(10):
            rhs = jnp.concatenate([wuv[4 * g + k] for k in range(4)], axis=0)
            at = [pl.ds(4 * g + k, NOWN, stride=H) for k in range(4)]
            lhs = jnp.concatenate([jnp.concatenate([ola[r, :], olb[r, :]], axis=1) for r in at], axis=0).astype(BF16)
            v = dot_t(lhs, rhs)
            o = v[3 * NOWN:]
            for k in range(3):
                o = jnp.where(lane256 // 64 == k, v[k * NOWN:(k + 1) * NOWN], o)
            groups.append(o.astype(BF16))
        heads = jnp.concatenate(groups, axis=1)
        weights[5].wait()
        mine = pl.ds(pl.multiple_of(core * NOWN, NOWN), NOWN)

        def xcopy(n):
            piece = xbuf.at[mine, pl.ds(n * 256, 256)]
            return pltpu.make_async_remote_copy(src_ref=piece, dst_ref=piece, send_sem=xs_sem.at[n], recv_sem=xr_sem.at[n],
                                                device_id={'cp': sibling}, device_id_type=pl.DeviceIdType.MESH)

        for n in range(10):
            xbuf[mine, n * 256:(n + 1) * 256] = dot(heads, wo[:, n * 256:(n + 1) * 256])
            if n >= 1:
                xcopy(n - 1).start()
        xcopy(9).start()
        for n in range(10):
            xcopy(n).wait_recv()
        xo_ref[...] = (x_ref[...].astype(F32) + xbuf[...]).astype(BF16)
        for n in range(10):
            xcopy(n).wait_send()

        def sent(i, _):
            rcopy_1(i).wait_send()
            rcopy_2(i).wait_send()
            return 0
        lax.fori_loop(0, NOWN, sent, 0)

    output()


def solution(mesh):
    half_dim = R // 2
    freq = 10000.0 ** (-2.0 * np.arange(half_dim, dtype=np.float64) / R)
    freq = np.tile(freq.astype(np.float32), 8)[None, :]

    def decode_step(x, w_dq, g_q, w_uq, w_dkv, g_kv, w_uk, w_uv, w_o, cache_c, cache_kr, ctx_len):
        vmem, hbm = pl.BlockSpec(memory_space=pltpu.VMEM), pl.BlockSpec(memory_space=pl.ANY)
        dma = pltpu.SemaphoreType.DMA
        part = pltpu.VMEM((NOWN + 1, 2 * H + 8, 128), F32)
        call = pl.pallas_call(
            decode_kernel,
            out_shape=(jax.ShapeDtypeStruct((NREQ, D), BF16), jax.ShapeDtypeStruct((NREQ, L), BF16), jax.ShapeDtypeStruct((NREQ, R), BF16)),
            in_specs=[vmem] * 5 + [pl.BlockSpec(memory_space=pltpu.SMEM)] + [hbm] * 8,
            out_specs=[vmem] * 3,
            scratch_shapes=[
                pltpu.VMEM((D, QL), BF16), pltpu.VMEM((QL, H * 96), BF16), pltpu.VMEM((L + R, D), BF16),
                pltpu.VMEM((H, 64, L), BF16), pltpu.VMEM((H, 64, L), BF16), pltpu.VMEM((H * 64, D), BF16),
                pltpu.VMEM((NB, T, L), BF16), pltpu.VMEM((NB, R, T), BF16),
                pltpu.VMEM((NREQ, H * 96), BF16), pltpu.VMEM((NREQ * H, 128), F32),
                pltpu.VMEM((NREQ, HP, L), BF16), pltpu.VMEM((NREQ, HP, 128), BF16),
                pltpu.VMEM((NREQ, L), F32), pltpu.VMEM((NREQ, 128), F32),
                pltpu.VMEM((2, H, T), F32), pltpu.VMEM((2, H, 128), F32), pltpu.VMEM((NCT, 256, 256), BF16),
                part, part, part, part, part,
                pltpu.VMEM((NREQ * H, 128), F32), pltpu.VMEM((NREQ * H, 128), F32), pltpu.VMEM((NREQ, D), F32),
                dma((6,)), dma((NB,)), dma((NB,)), dma((NOWN,)), dma((NOWN,)), dma((NOWN,)), dma((NOWN,)), dma((10,)), dma((10,)),
            ],
            compiler_params=pltpu.CompilerParams(collective_id=0, has_side_effects=True, vmem_limit_bytes=67_043_328),
        )
        ctx_cols = jnp.broadcast_to(ctx_len[:, None], (NREQ, 128))
        return call(x, g_q[None, :], g_kv[None, :], jnp.asarray(freq), ctx_cols, ctx_len, w_dq, w_uq, w_dkv.T,
                    jnp.transpose(w_uk, (1, 2, 0)), jnp.transpose(w_uv, (1, 2, 0)), w_o, cache_c, jnp.swapaxes(cache_kr, 1, 2))

    rows, cache = P('dp', None), P('dp', 'cp', None)
    in_specs = (rows, P(), P(), P(), P(), P(), P(), P(), P(), cache, cache, P('dp'))
    return jax.shard_map(decode_step, mesh=mesh, in_specs=in_specs, out_specs=(rows, rows, rows), check_vma=False)
```

time: 360 us -> 94.7 us (0.26)
  matrix products: 179 us -> 0 us
  waiting for transfers between devices: 101 us -> 0 us
  Pallas kernels: 0 us -> 86.7 us
  other arithmetic: 53.6 us -> 0 us
  between operations: 14.4 us -> 0.64 us
  local copies, waits for them, and re-layouts: 12.4 us -> 7.09 us
    dot_general x11 -> x0, matrix products: 179 us -> none  [the longest x1 71.8 us: block_partials(): jnp.einsum('bhk,btk->bht', q_lat, cache_c, preferred_element_type=jnp.flo...]
    all_gather x1 -> x0, waiting for transfers between devices: 100 us -> none  [decode_step(): gathered = lax.all_gather(packed, 'cp')]
    pallas_call x0 -> x1, Pallas kernels: none -> 86.7 us  [decode_step(): call(x, g_q[None, :], g_kv[None, :], jnp.asarray(freq), ctx_cols, ctx_len...]
    reduce_sum x4 -> x0, other arithmetic: 35 us -> none  [the longest x1 26.7 us: block_partials(): row_sum = jnp.sum(weights, axis=2) + new_weight]
    slice x1 -> x0, other arithmetic: 9.68 us -> none  [decode_step(): mass_sum = jnp.sum(factor * gathered[:, :, :, 1], axis=0)]
    concatenate x3 -> x0, other arithmetic: 6.03 us -> none  [the longest x1 5.41 us: decode_step(): jnp.concatenate([row_max[:, :, None], row_sum[:, :, None], lat_acc], axis=2)]
    slice x3 -> x0, local copies, waits for them, and re-layouts: 3.77 us -> none  [the longest x1 3.45 us: decode_step(): mass_sum = jnp.sum(factor * gathered[:, :, :, 1], axis=0)]
  transfers between devices with their start and end apart: 1 -> 0, of which waited for: 1 -> 0; matrix products, arithmetic and copies ran while one was open for 0% -> 0% of each run, Pallas kernels for 0% -> 0%
where the time goes in v1:
time: 94.7 us; the launch traced here: 94.4 us
  Pallas kernels  86.7 us (92%)
  local copies, waits for them, and re-layouts  7.09 us (7%)
    pallas_call x1, Pallas kernels, decode_step(): call(x, g_q[None, :], g_kv[None, :], jnp.asarray(freq), ctx_cols, ctx_len...  86.7 us
    unnamed x2, local copies, waits for them, and re-layouts  3.09 us

profile of v1, /device:TPU:0, one launch (start us, length us, event | category | flops | bytes accessed | tf_op | source)
XLA Modules:
  0.0 94.4 jit_solution(12832970103476150093)
XLA Ops:
  0.6 1.3 %broadcast_in_dim.12.gq_ref = f32[1,768]{1,0:T(1,128)} reshape(f32[768]{0:T(1024)} %param.15) | data formatting | bytes 6144 | tf_op jit(solution)/shard_map/broadcast_in_dim | solution.py:373
  1.9 1.3 %broadcast_in_dim.14.ctxv_ref = s32[64,128]{1,0:T(8,128)} broadcast(s32[64]{0:T(128)} %ctx_ref.1), dimensions={0} | broadcast | bytes 33024 | tf_op jit(solution)/shard_map/broadcast_in_dim | solution.py:372
  3.2 86.7 %shard_map.148 = (bf16[64,2560]{1,0:T(8,128)(2,1)}, bf16[64,256]{1,0:T(8,128)(2,1)}, bf16[64,32]{1,0:T(8,128)(2,1)}) custom-call(bf16[64,2560]{1,0:T(8,128)(2,1)} %x_ref.1, f32[1,768]{1,0:T(1,128)} %broadcast_in_dim.12.gq_ref, f32[1,256]{1,0:T(1,128)} %bitcast.9, f32[1,128]{1,0:T(1,128)} %constant.2.clone.freq_ref, s32[64,128]{1,0:T(8,128)} %broadcast_in_dim.14.ctxv_ref, ...), custom_call_target="tpu_custom_call" | custom-call | tf_op jit(solution)/shard_map/pallas_call | solution.py:373
  90.0 1.4 %copy.16 = bf16[64,32]{0,1:T(8,128)(2,1)} copy(bf16[64,32]{1,0:T(8,128)(2,1)} %get-tuple-element.5) | data formatting | bytes 8192 | tf_op jit(solution)/shard_map/pallas_call | solution.py:373
  91.3 1.7 %copy.19 = bf16[64,2560]{1,0:T(8,128)(2,1)} copy(bf16[64,2560]{1,0:T(8,128)(2,1)} %get-tuple-element.9) | data formatting | bytes 655360
  93.1 1.4 %copy.20 = bf16[64,256]{1,0:T(8,128)(2,1)} copy(bf16[64,256]{1,0:T(8,128)(2,1)} %get-tuple-element.10) | data formatting | bytes 65536

commit v2 on v1

--- a/solution.py
+++ b/solution.py
@@ -19,14 +19,14 @@
 NT = 8
 NB = 8
 NOWN = NREQ // 2
-LEAD = 3
+LEAD = 1
 NCT = 8
 XPOSE_TILES = ((1, 0), (0, 0))
 
 
-def decode_kernel(x_ref, gq_ref, gkv_ref, freq_ref, ctxv_ref, ctx_ref, wdq_h, wuq_h, wdkv_h, wuk_h, wuv_h, wo_h, c_h, kr_h,
+def decode_kernel(x_ref, gq_ref, gkv_ref, freq_ref, ctx_ref, wdq_h, wuq_h, wdkv_h, wuk_h, wuv_h, wo_h, c_h, kr_h,
                   xo_ref, co_ref, ko_ref,
-                  wdq, wuq, wdkv, wuk, wuv, wo, cbuf, krbuf, qf, qrf, qb, qrb, cnf, krf,
+                  wdq, wuq, wdkv, wuk, wuv, wo, cbuf, krbuf, qf, qla, qlb, qrf, qb, qrb, cnf, krf, ctxv,
                   sbuf, mbuf, ctb, send_a, recv_1, own_b, send_b, recv_2, ola, olb, xbuf,
                   wsem, csem, ksem, sa_sem, r1_sem, sb_sem, r2_sem, xs_sem, xr_sem):
     cp = lax.axis_index('cp')
@@ -61,8 +61,6 @@
 
     for copy in weights[:4]:
         copy.start()
-    for s in range(NB):
-        start(s)
 
     lane128 = lax.broadcasted_iota(jnp.int32, (1, 128), 1)
     lane256 = lax.broadcasted_iota(jnp.int32, (1, 256), 1)
@@ -70,7 +68,11 @@
     dot = functools.partial(jnp.dot, preferred_element_type=F32)
     dot_t = functools.partial(lax.dot_general, dimension_numbers=(((1,), (1,)), ((), ())), preferred_element_type=F32)
 
-    angle = ctxv_ref[...].astype(F32) * freq_ref[...]
+    def fill(b, _):
+        ctxv[pl.ds(b, 1), :] = jnp.full((1, 128), ctx_ref[b], jnp.int32)
+        return 0
+    lax.fori_loop(0, NREQ, fill, 0)
+    angle = ctxv[...].astype(F32) * freq_ref[...]
     cos_t = jnp.cos(angle)
     sin_t = jnp.sin(angle) * jnp.where(lax.rem(lane128, 32) < 16, -1.0, 1.0)
 
@@ -78,22 +80,24 @@
     cq = [dot(x_ref[...], wdq[:, n * 256:(n + 1) * 256]).astype(BF16).astype(F32) for n in range(3)]
     mean_sq = sum(jnp.sum(v * v, axis=1, keepdims=True) for v in cq) * np.float32(1.0 / QL)
     inv_q = lax.rsqrt(mean_sq + NORM_EPS)
-    cn = jnp.concatenate([(cq[n] * inv_q * gq_ref[:, n * 256:(n + 1) * 256]).astype(BF16) for n in range(3)], axis=1)
+    cn = jnp.concatenate([(cq[n] * inv_q * gq_ref[n * 256:(n + 1) * 256][None, :]).astype(BF16) for n in range(3)], axis=1)
 
     weights[1].wait()
     kv = dot_t(x_ref[...], wdkv[:L, :])
     inv_kv = lax.rsqrt(jnp.sum(kv * kv, axis=1, keepdims=True) * np.float32(1.0 / L) + NORM_EPS)
-    c_new = (kv * inv_kv * gkv_ref[...]).astype(BF16)
+    c_new = (kv * inv_kv * gkv_ref[...][None, :]).astype(BF16)
     co_ref[...] = c_new
     cnf[...] = c_new.astype(F32)
     kr = dot_t(x_ref[...], wdkv[L:L + R, :])
     kr = jnp.concatenate([kr, jnp.zeros((NREQ, 128 - R), F32)], axis=1)
     partner = jnp.where(lane128 < 16, pltpu.roll(kr, 112, 1), pltpu.roll(kr, 16, 1))
     kr_new = (kr * cos_t + partner * sin_t).astype(BF16)
-    ko_ref[...] = kr_new[:, :R]
+    ko_ref[...] = jnp.where(lane128 < R, kr_new, jnp.zeros_like(kr_new))
     krf[...] = jnp.where(lane128 < R, kr_new.astype(F32), 0.0)
 
     weights[2].wait()
+    for s in range(NB):
+        start(s)
     for n in range(15):
         qf[:, n * 256:(n + 1) * 256] = dot(cn, wuq[:, n * 256:(n + 1) * 256]).astype(BF16)
 
@@ -134,16 +138,12 @@
                 carry[h] = v
                 continue
             v = v.astype(BF16).astype(F32)
-            ola[pl.ds(h, NREQ, stride=H), :] = v[:, :128]
-            olb[pl.ds(h, NREQ, stride=H), :] = v[:, 128:]
+            qla[pl.ds(h, NREQ, stride=H), :] = v[:, :128]
+            qlb[pl.ds(h, NREQ, stride=H), :] = v[:, 128:]
     pl.semaphore_wait(barrier, 2)
 
-    def to_bf16(b, _):
-        rows = pl.ds(pl.multiple_of(b * H, 8), H)
-        qb[b] = jnp.concatenate([jnp.concatenate([ola[rows, :], olb[rows, :]], axis=1), jnp.zeros((HP - H, L), F32)], axis=0).astype(BF16)
-        qrb[b] = jnp.concatenate([qrf[rows, :], jnp.zeros((HP - H, 128), F32)], axis=0).astype(BF16)
-        return 0
-    lax.fori_loop(0, NREQ, to_bf16, 0)
+    def head_rows(i):
+        return pl.ds(pl.multiple_of(i * H, 8), H)
 
     def rcopy_1(i):
         return pltpu.make_async_remote_copy(src_ref=send_a.at[i], dst_ref=recv_1.at[i], send_sem=sa_sem.at[i], recv_sem=r1_sem.at[i],
@@ -180,19 +180,25 @@
         ii = jnp.minimum(i, NOWN - 1)
         b = core * NOWN + ii
         c_row, k_row = cnf[pl.ds(b, 1), :], krf[pl.ds(b, 1), :]
-        q, qr = qb[b].astype(F32)[:H], qrb[b].astype(F32)[:H]
-        part = q[:, :128] * c_row[:, :128] + q[:, 128:] * c_row[:, 128:] + qr * k_row
+        mine = head_rows(b)
+        part = qla[mine, :] * c_row[:, :128] + qlb[mine, :] * c_row[:, 128:] + qrf[mine, :] * k_row
         s_new = jnp.broadcast_to(jnp.sum(part, axis=1, keepdims=True) * SCALE, (H, 128))
         m = jnp.maximum(jnp.maximum(m_p, m_q), s_new)
         f_p, f_q, w_new = jnp.exp2(m_p - m), jnp.exp2(m_q - m), jnp.exp2(s_new - m)
         inv = 1.0 / (l_p * f_p + l_q * f_q + w_new)
         w_new = w_new.astype(BF16).astype(F32)
-        rows = pl.ds(pl.multiple_of(i * H, 8), H)
+        rows = head_rows(i)
         ola[rows, :] = (lo_p * f_p + lo_q * f_q + w_new * c_row[:, :128]) * inv
         olb[rows, :] = (hi_p * f_p + hi_q * f_q + w_new * c_row[:, 128:]) * inv
 
     def attend():
         count = [0]
+
+        def load_q(s, par):
+            rows = head_rows(request(s))
+            q = jnp.concatenate([qla[rows, :], qlb[rows, :]], axis=1)
+            qb[par] = jnp.concatenate([q, jnp.zeros((HP - H, L), F32)], axis=0).astype(BF16)
+            qrb[par] = jnp.concatenate([qrf[rows, :], jnp.zeros((HP - H, 128), F32)], axis=0).astype(BF16)
 
         def qk_tile(s, par, j, mx):
             slot, b = lax.rem(s, NB), request(s)
@@ -200,13 +206,13 @@
             at = pl.ds(256 * j, 256)
             c = cbuf[slot, at, :]
             if (par, j // 2) in XPOSE_TILES:
-                v = dot_t(qb[b], c)
+                v = dot_t(qb[par], c)
             else:
                 t = count[0] % NCT
                 count[0] += 1
                 ctb[t] = c.T
-                v = dot(qb[b], ctb[t])
-            v = (v + dot(qrb[b][:, :R], krbuf[slot, :, at]))[:H]
+                v = dot(qb[par], ctb[t])
+            v = (v + dot(qrb[par, :, :R], krbuf[slot, :, at]))[:H]
             v = jnp.where(lane256 + j * 256 < n, v, MASKED)
             sbuf[par, :, at] = v
             for k in range(2):
@@ -227,6 +233,8 @@
         def half(s, par, out, out_i, last=False):
             mk = jnp.broadcast_to(jnp.maximum(jnp.max(mbuf[par], axis=1, keepdims=True), FLOOR) * SCALE, (H, 128))
             mx, st = None, {0: None, 1: None, 'l': None}
+            if not last:
+                load_q(s + 1, 1 - par)
             for j in range(2 * (NT + LEAD)):
                 if not last and j < 2 * NT:
                     mx = qk_tile(s + 1, 1 - par, j, mx)
@@ -242,6 +250,7 @@
             ref[NOWN] = jnp.zeros((2 * H + 8, 128), F32)
 
         wait(0)
+        load_q(0, 0)
         mx = None
         for j in range(2 * NT):
             mx = qk_tile(0, 0, j, mx)
@@ -341,6 +350,12 @@
     output()
 
 
+def finish_kernel(x_ref, c_ref, k_ref, xo_ref, co_ref, ko_ref):
+    xo_ref[...] = x_ref[...]
+    co_ref[...] = c_ref[...]
+    ko_ref[...] = k_ref[...].astype(F32).T[:R].astype(BF16)
+
+
 def solution(mesh):
     half_dim = R // 2
     freq = 10000.0 ** (-2.0 * np.arange(half_dim, dtype=np.float64) / R)
@@ -352,26 +367,28 @@
         part = pltpu.VMEM((NOWN + 1, 2 * H + 8, 128), F32)
         call = pl.pallas_call(
             decode_kernel,
-            out_shape=(jax.ShapeDtypeStruct((NREQ, D), BF16), jax.ShapeDtypeStruct((NREQ, L), BF16), jax.ShapeDtypeStruct((NREQ, R), BF16)),
-            in_specs=[vmem] * 5 + [pl.BlockSpec(memory_space=pltpu.SMEM)] + [hbm] * 8,
+            out_shape=(jax.ShapeDtypeStruct((NREQ, D), BF16), jax.ShapeDtypeStruct((NREQ, L), BF16), jax.ShapeDtypeStruct((NREQ, 128), BF16)),
+            in_specs=[vmem] * 4 + [pl.BlockSpec(memory_space=pltpu.SMEM)] + [hbm] * 8,
             out_specs=[vmem] * 3,
             scratch_shapes=[
                 pltpu.VMEM((D, QL), BF16), pltpu.VMEM((QL, H * 96), BF16), pltpu.VMEM((L + R, D), BF16),
                 pltpu.VMEM((H, 64, L), BF16), pltpu.VMEM((H, 64, L), BF16), pltpu.VMEM((H * 64, D), BF16),
                 pltpu.VMEM((NB, T, L), BF16), pltpu.VMEM((NB, R, T), BF16),
-                pltpu.VMEM((NREQ, H * 96), BF16), pltpu.VMEM((NREQ * H, 128), F32),
-                pltpu.VMEM((NREQ, HP, L), BF16), pltpu.VMEM((NREQ, HP, 128), BF16),
-                pltpu.VMEM((NREQ, L), F32), pltpu.VMEM((NREQ, 128), F32),
+                pltpu.VMEM((NREQ, H * 96), BF16), pltpu.VMEM((NREQ * H, 128), F32), pltpu.VMEM((NREQ * H, 128), F32), pltpu.VMEM((NREQ * H, 128), F32),
+                pltpu.VMEM((2, HP, L), BF16), pltpu.VMEM((2, HP, 128), BF16),
+                pltpu.VMEM((NREQ, L), F32), pltpu.VMEM((NREQ, 128), F32), pltpu.VMEM((NREQ, 128), jnp.int32),
                 pltpu.VMEM((2, H, T), F32), pltpu.VMEM((2, H, 128), F32), pltpu.VMEM((NCT, 256, 256), BF16),
                 part, part, part, part, part,
-                pltpu.VMEM((NREQ * H, 128), F32), pltpu.VMEM((NREQ * H, 128), F32), pltpu.VMEM((NREQ, D), F32),
+                pltpu.VMEM(((NOWN + 1) * H, 128), F32), pltpu.VMEM(((NOWN + 1) * H, 128), F32), pltpu.VMEM((NREQ, D), F32),
                 dma((6,)), dma((NB,)), dma((NB,)), dma((NOWN,)), dma((NOWN,)), dma((NOWN,)), dma((NOWN,)), dma((10,)), dma((10,)),
             ],
             compiler_params=pltpu.CompilerParams(collective_id=0, has_side_effects=True, vmem_limit_bytes=67_043_328),
         )
-        ctx_cols = jnp.broadcast_to(ctx_len[:, None], (NREQ, 128))
-        return call(x, g_q[None, :], g_kv[None, :], jnp.asarray(freq), ctx_cols, ctx_len, w_dq, w_uq, w_dkv.T,
+        outs = call(x, g_q, g_kv, jnp.asarray(freq), ctx_len, w_dq, w_uq, w_dkv.T,
                     jnp.transpose(w_uk, (1, 2, 0)), jnp.transpose(w_uv, (1, 2, 0)), w_o, cache_c, jnp.swapaxes(cache_kr, 1, 2))
+        shapes = [jax.ShapeDtypeStruct(shape, BF16) for shape in ((NREQ, D), (NREQ, L), (R, NREQ))]
+        x_out, c_new, kr_new = pl.pallas_call(finish_kernel, out_shape=shapes, in_specs=[vmem] * 3, out_specs=[vmem] * 3)(*outs)
+        return x_out, c_new, kr_new.T
 
     rows, cache = P('dp', None), P('dp', 'cp', None)
     in_specs = (rows, P(), P(), P(), P(), P(), P(), P(), P(), cache, cache, P('dp'))

time: 94.7 us -> 84.4 us (0.89)
  local copies, waits for them, and re-layouts: 7.09 us -> 0 us
  Pallas kernels: 86.7 us -> 83.6 us
    pallas_call x1 -> x2, Pallas kernels: 86.7 us -> 83.6 us  [the longest x1 81.9 us: decode_step(): call(x, g_q, g_kv, jnp.asarray(freq), ctx_len, w_dq, w_uq, w_dkv.T, jnp.t...]
    unnamed x2 -> x0, local copies, waits for them, and re-layouts: 3.09 us -> none
    broadcast_in_dim x2 -> x0, local copies, waits for them, and re-layouts: 2.61 us -> none  [the longest x1 1.34 us: decode_step(): ctx_cols = jnp.broadcast_to(ctx_len[:, None], (NREQ, 128))]
    pallas_call x1 -> x0, local copies, waits for them, and re-layouts: 1.39 us -> none  [decode_step(): call(x, g_q[None, :], g_kv[None, :], jnp.asarray(freq), ctx_cols, ctx_len...]
where the time goes in v2:
time: 84.4 us; the launch traced here: 84.3 us
  Pallas kernels  83.6 us (99%)
    pallas_call x1, Pallas kernels, decode_step(): call(x, g_q, g_kv, jnp.asarray(freq), ctx_len, w_dq, w_uq, w_dkv.T, jnp.t...  81.9 us
    pallas_call x1, Pallas kernels, decode_step(): pl.pallas_call(finish_kernel, out_shape=shapes, in_specs=[vmem] * 3, out_...  1.75 us

profile of v2, /device:TPU:0, one launch (start us, length us, event | category | flops | bytes accessed | tf_op | source)
XLA Modules:
  0.0 84.3 jit_solution(11065236398774943510)
XLA Ops:
  0.6 81.9 %shard_map.148 = (bf16[64,2560]{1,0:T(8,128)(2,1)}, bf16[64,256]{1,0:T(8,128)(2,1)}, bf16[64,128]{1,0:T(8,128)(2,1)}) custom-call(bf16[64,2560]{1,0:T(8,128)(2,1)} %x_ref.1, f32[768]{0:T(1024)} %gq_ref.1, f32[256]{0:T(256)} %gkv_ref.1, f32[1,128]{1,0:T(1,128)} %constant.2.clone.freq_ref, s32[64]{0:T(128)} %ctx_ref.1, bf16[2560,768]{1,0:T(8,128)(2,1)} %wdq_h.1, ...), custom_call_target="tpu_custom_call" | custom-call | tf_op jit(solution)/shard_map/pallas_call | solution.py:387
  82.5 1.7 %shard_map.149 = (bf16[64,2560]{1,0:T(8,128)(2,1)}, bf16[64,256]{1,0:T(8,128)(2,1)}, bf16[32,64]{1,0:T(8,128)(2,1)}) custom-call(bf16[64,2560]{1,0:T(8,128)(2,1)} %get-tuple-element.9.x_ref, bf16[64,256]{1,0:T(8,128)(2,1)} %get-tuple-element.10.c_ref, bf16[64,128]{1,0:T(8,128)(2,1)} %get-tuple-element.11.k_ref), custom_call_target="tpu_custom_call" | custom-call | tf_op jit(solution)/shard_map/pallas_call | solution.py:390

commit v3 on v2

--- a/solution.py
+++ b/solution.py
@@ -275,6 +275,11 @@
             lagged = lambda lag: jnp.where(i >= lag, i - lag, NOWN)
             half(s, 0, send_a, i)
             combine_1(lagged(2))
+            if last:
+                rcopy_1(i).start()
+                rcopy_1(i - 1).wait_recv()
+                combine_1(i - 1)
+                rcopy_2(i - 2).start()
             half(s + 1, 1, own_b, i, last=last)
             combine_2(lagged(6))
 
@@ -291,21 +296,14 @@
             return 0
         lax.fori_loop(0, NOWN - 1, loop_trip, 0)
         trip(NOWN - 1, last=True)
-        rcopy_1(NOWN - 1).start()
-        rcopy_1(NOWN - 2).wait_recv()
-        combine_1(NOWN - 2)
-        rcopy_2(NOWN - 3).start()
         rcopy_1(NOWN - 1).wait_recv()
         rcopy_2(NOWN - 2).start()
         combine_1(NOWN - 1)
-        for i in range(NOWN - 6, NOWN - 3):
+        for i in range(NOWN - 6, NOWN):
             rcopy_2(i).wait_recv()
+            combine_2(i)
             if i == NOWN - 6:
                 rcopy_2(NOWN - 1).start()
-            combine_2(i)
-        for i in range(NOWN - 3, NOWN):
-            rcopy_2(i).wait_recv()
-            combine_2(i)
 
     attend()
 
@@ -326,19 +324,18 @@
         mine = pl.ds(pl.multiple_of(core * NOWN, NOWN), NOWN)
 
         def xcopy(n):
-            piece = xbuf.at[mine, pl.ds(n * 256, 256)]
+            piece = xbuf.at[mine, pl.ds(n * 1280, 1280)]
             return pltpu.make_async_remote_copy(src_ref=piece, dst_ref=piece, send_sem=xs_sem.at[n], recv_sem=xr_sem.at[n],
                                                 device_id={'cp': sibling}, device_id_type=pl.DeviceIdType.MESH)
 
-        for n in range(10):
-            xbuf[mine, n * 256:(n + 1) * 256] = dot(heads, wo[:, n * 256:(n + 1) * 256])
-            if n >= 1:
-                xcopy(n - 1).start()
-        xcopy(9).start()
-        for n in range(10):
+        for n in range(2):
+            for k in range(5 * n, 5 * n + 5):
+                xbuf[mine, k * 256:(k + 1) * 256] = dot(heads, wo[:, k * 256:(k + 1) * 256])
+            xcopy(n).start()
+        for n in range(2):
             xcopy(n).wait_recv()
         xo_ref[...] = (x_ref[...].astype(F32) + xbuf[...]).astype(BF16)
-        for n in range(10):
+        for n in range(2):
             xcopy(n).wait_send()
 
         def sent(i, _):

time: 84.4 us -> 82.3 us (0.975)
  Pallas kernels: 83.6 us -> 81.5 us
    pallas_call x1, Pallas kernels: 81.9 us -> 79.8 us  [decode_step(): call(x, g_q, g_kv, jnp.asarray(freq), ctx_len, w_dq, w_uq, w_dkv.T, jnp.t...]
where the time goes in v3:
time: 82.3 us; the launch traced here: 82.2 us
  Pallas kernels  81.5 us (99%)
    pallas_call x1, Pallas kernels, decode_step(): call(x, g_q, g_kv, jnp.asarray(freq), ctx_len, w_dq, w_uq, w_dkv.T, jnp.t...  79.8 us
    pallas_call x1, Pallas kernels, decode_step(): pl.pallas_call(finish_kernel, out_shape=shapes, in_specs=[vmem] * 3, out_...  1.75 us

profile of v3, /device:TPU:0, one launch (start us, length us, event | category | flops | bytes accessed | tf_op | source)
XLA Modules:
  0.0 82.2 jit_solution(1001840108986933359)
XLA Ops:
  0.6 79.8 %shard_map.148 = (bf16[64,2560]{1,0:T(8,128)(2,1)}, bf16[64,256]{1,0:T(8,128)(2,1)}, bf16[64,128]{1,0:T(8,128)(2,1)}) custom-call(bf16[64,2560]{1,0:T(8,128)(2,1)} %x_ref.1, f32[768]{0:T(1024)} %gq_ref.1, f32[256]{0:T(256)} %gkv_ref.1, f32[1,128]{1,0:T(1,128)} %constant.2.clone.freq_ref, s32[64]{0:T(128)} %ctx_ref.1, bf16[2560,768]{1,0:T(8,128)(2,1)} %wdq_h.1, ...), custom_call_target="tpu_custom_call" | custom-call | tf_op jit(solution)/shard_map/pallas_call | solution.py:384
  80.4 1.7 %shard_map.149 = (bf16[64,2560]{1,0:T(8,128)(2,1)}, bf16[64,256]{1,0:T(8,128)(2,1)}, bf16[32,64]{1,0:T(8,128)(2,1)}) custom-call(bf16[64,2560]{1,0:T(8,128)(2,1)} %get-tuple-element.9.x_ref, bf16[64,256]{1,0:T(8,128)(2,1)} %get-tuple-element.10.c_ref, bf16[64,128]{1,0:T(8,128)(2,1)} %get-tuple-element.11.k_ref), custom_call_target="tpu_custom_call" | custom-call | tf_op jit(solution)/shard_map/pallas_call | solution.py:387

commit v4 on v3

--- a/solution.py
+++ b/solution.py
@@ -19,15 +19,14 @@
 NT = 8
 NB = 8
 NOWN = NREQ // 2
-LEAD = 1
-NCT = 8
+LEAD = 4
 XPOSE_TILES = ((1, 0), (0, 0))
 
 
 def decode_kernel(x_ref, gq_ref, gkv_ref, freq_ref, ctx_ref, wdq_h, wuq_h, wdkv_h, wuk_h, wuv_h, wo_h, c_h, kr_h,
                   xo_ref, co_ref, ko_ref,
                   wdq, wuq, wdkv, wuk, wuv, wo, cbuf, krbuf, qf, qla, qlb, qrf, qb, qrb, cnf, krf, ctxv,
-                  sbuf, mbuf, ctb, send_a, recv_1, own_b, send_b, recv_2, ola, olb, xbuf,
+                  sbuf, mbuf, send_a, recv_1, own_b, send_b, recv_2, ola, olb, xbuf,
                   wsem, csem, ksem, sa_sem, r1_sem, sb_sem, r2_sem, xs_sem, xr_sem):
     cp = lax.axis_index('cp')
     core = lax.rem(cp, 2)
@@ -192,8 +191,6 @@
         olb[rows, :] = (hi_p * f_p + hi_q * f_q + w_new * c_row[:, 128:]) * inv
 
     def attend():
-        count = [0]
-
         def load_q(s, par):
             rows = head_rows(request(s))
             q = jnp.concatenate([qla[rows, :], qlb[rows, :]], axis=1)
@@ -208,10 +205,7 @@
             if (par, j // 2) in XPOSE_TILES:
                 v = dot_t(qb[par], c)
             else:
-                t = count[0] % NCT
-                count[0] += 1
-                ctb[t] = c.T
-                v = dot(qb[par], ctb[t])
+                v = dot(qb[par], jnp.concatenate([c[:, :128].T, c[:, 128:].T], axis=0))
             v = (v + dot(qrb[par, :, :R], krbuf[slot, :, at]))[:H]
             v = jnp.where(lane256 + j * 256 < n, v, MASKED)
             sbuf[par, :, at] = v
@@ -374,7 +368,7 @@
                 pltpu.VMEM((NREQ, H * 96), BF16), pltpu.VMEM((NREQ * H, 128), F32), pltpu.VMEM((NREQ * H, 128), F32), pltpu.VMEM((NREQ * H, 128), F32),
                 pltpu.VMEM((2, HP, L), BF16), pltpu.VMEM((2, HP, 128), BF16),
                 pltpu.VMEM((NREQ, L), F32), pltpu.VMEM((NREQ, 128), F32), pltpu.VMEM((NREQ, 128), jnp.int32),
-                pltpu.VMEM((2, H, T), F32), pltpu.VMEM((2, H, 128), F32), pltpu.VMEM((NCT, 256, 256), BF16),
+                pltpu.VMEM((2, H, T), F32), pltpu.VMEM((2, H, 128), F32),
                 part, part, part, part, part,
                 pltpu.VMEM(((NOWN + 1) * H, 128), F32), pltpu.VMEM(((NOWN + 1) * H, 128), F32), pltpu.VMEM((NREQ, D), F32),
                 dma((6,)), dma((NB,)), dma((NB,)), dma((NOWN,)), dma((NOWN,)), dma((NOWN,)), dma((NOWN,)), dma((10,)), dma((10,)),

time: 82.3 us -> 80.9 us (0.983)
  Pallas kernels: 81.5 us -> 80.1 us
    pallas_call x1, Pallas kernels: 79.8 us -> 78.4 us  [decode_step(): call(x, g_q, g_kv, jnp.asarray(freq), ctx_len, w_dq, w_uq, w_dkv.T, jnp.t...]
where the time goes in v4:
time: 80.9 us; the launch traced here: 80.8 us
  Pallas kernels  80.1 us (99%)
    pallas_call x1, Pallas kernels, decode_step(): call(x, g_q, g_kv, jnp.asarray(freq), ctx_len, w_dq, w_uq, w_dkv.T, jnp.t...  78.4 us
    pallas_call x1, Pallas kernels, decode_step(): pl.pallas_call(finish_kernel, out_shape=shapes, in_specs=[vmem] * 3, out_...  1.75 us

profile of v4, /device:TPU:0, one launch (start us, length us, event | category | flops | bytes accessed | tf_op | source)
XLA Modules:
  0.0 80.8 jit_solution(5211063646614466766)
XLA Ops:
  0.6 78.4 %shard_map.148 = (bf16[64,2560]{1,0:T(8,128)(2,1)}, bf16[64,256]{1,0:T(8,128)(2,1)}, bf16[64,128]{1,0:T(8,128)(2,1)}) custom-call(bf16[64,2560]{1,0:T(8,128)(2,1)} %x_ref.1, f32[768]{0:T(1024)} %gq_ref.1, f32[256]{0:T(256)} %gkv_ref.1, f32[1,128]{1,0:T(1,128)} %constant.2.clone.freq_ref, s32[64]{0:T(128)} %ctx_ref.1, bf16[2560,768]{1,0:T(8,128)(2,1)} %wdq_h.1, ...), custom_call_target="tpu_custom_call" | custom-call | tf_op jit(solution)/shard_map/pallas_call | solution.py:378
  79.0 1.7 %shard_map.149 = (bf16[64,2560]{1,0:T(8,128)(2,1)}, bf16[64,256]{1,0:T(8,128)(2,1)}, bf16[32,64]{1,0:T(8,128)(2,1)}) custom-call(bf16[64,2560]{1,0:T(8,128)(2,1)} %get-tuple-element.9.x_ref, bf16[64,256]{1,0:T(8,128)(2,1)} %get-tuple-element.10.c_ref, bf16[64,128]{1,0:T(8,128)(2,1)} %get-tuple-element.11.k_ref), custom_call_target="tpu_custom_call" | custom-call | tf_op jit(solution)/shard_map/pallas_call | solution.py:381

commit v5 on v4

--- a/solution.py
+++ b/solution.py
@@ -20,7 +20,7 @@
 NB = 8
 NOWN = NREQ // 2
 LEAD = 4
-XPOSE_TILES = ((1, 0), (0, 0))
+XPOSE_TILES = ((1, 0), (0, 1))
 
 
 def decode_kernel(x_ref, gq_ref, gkv_ref, freq_ref, ctx_ref, wdq_h, wuq_h, wdkv_h, wuk_h, wuv_h, wo_h, c_h, kr_h,

time: 80.9 us -> 80.7 us (level)
  no operation moved by 1% of the time
where the time goes in v5:
time: 80.7 us; the launch traced here: 80.5 us
  Pallas kernels  79.9 us (99%)
    pallas_call x1, Pallas kernels, decode_step(): call(x, g_q, g_kv, jnp.asarray(freq), ctx_len, w_dq, w_uq, w_dkv.T, jnp.t...  78.2 us
    pallas_call x1, Pallas kernels, decode_step(): pl.pallas_call(finish_kernel, out_shape=shapes, in_specs=[vmem] * 3, out_...  1.75 us

profile of v5, /device:TPU:0, one launch (start us, length us, event | category | flops | bytes accessed | tf_op | source)
XLA Modules:
  0.0 80.5 jit_solution(14465468599953531874)
XLA Ops:
  0.6 78.2 %shard_map.148 = (bf16[64,2560]{1,0:T(8,128)(2,1)}, bf16[64,256]{1,0:T(8,128)(2,1)}, bf16[64,128]{1,0:T(8,128)(2,1)}) custom-call(bf16[64,2560]{1,0:T(8,128)(2,1)} %x_ref.1, f32[768]{0:T(1024)} %gq_ref.1, f32[256]{0:T(256)} %gkv_ref.1, f32[1,128]{1,0:T(1,128)} %constant.2.clone.freq_ref, s32[64]{0:T(128)} %ctx_ref.1, bf16[2560,768]{1,0:T(8,128)(2,1)} %wdq_h.1, ...), custom_call_target="tpu_custom_call" | custom-call | tf_op jit(solution)/shard_map/pallas_call | solution.py:378
  78.8 1.7 %shard_map.149 = (bf16[64,2560]{1,0:T(8,128)(2,1)}, bf16[64,256]{1,0:T(8,128)(2,1)}, bf16[32,64]{1,0:T(8,128)(2,1)}) custom-call(bf16[64,2560]{1,0:T(8,128)(2,1)} %get-tuple-element.9.x_ref, bf16[64,256]{1,0:T(8,128)(2,1)} %get-tuple-element.10.c_ref, bf16[64,128]{1,0:T(8,128)(2,1)} %get-tuple-element.11.k_ref), custom_call_target="tpu_custom_call" | custom-call | tf_op jit(solution)/shard_map/pallas_call | solution.py:381
